TPU v7x, 32 devices: a whole 2x2x4 slice. The times are simulated.
32 devices in a mesh: dp: 4 (over y, x), ctx: 8 (over z, core).
Axes of the slice: x: 2, y: 2, z: 4, core: 2. Of those that a mesh axis runs over, the one named last changes fastest.
Arguments:
- layer_input: bfloat16 [4, 1024, 7168], P(None, 'ctx', 'dp'), may hold values from -6 to 6
- kv_latent: bfloat16 [4, 1024, 512], P('dp', 'ctx'), may hold values from -8 to 8
- key_rope: bfloat16 [4, 1024, 64], P('dp', 'ctx'), may hold values from -6 to 6
- q_latent: bfloat16 [4, 1024, 8, 512], P('dp', 'ctx'), may hold values from -60 to 60
- q_rope: bfloat16 [4, 1024, 8, 64], P('dp', 'ctx'), may hold values from -3 to 3
- saved_output: bfloat16 [4, 1024, 8, 512], P('dp', 'ctx'), may hold values from -4 to 4
- w_uv: bfloat16 [512, 1024], replicated, may hold values from -0.25 to 0.25
- d_out: bfloat16 [4, 1024, 1024], P('dp', 'ctx'), may hold values from -6 to 6
- blocks: int32 [16], replicated, may hold values from 0 to 15, each once
Outputs:
- d_q_latent: bfloat16 [4, 1024, 8, 512], P('dp', 'ctx')
- d_q_rope: bfloat16 [4, 1024, 8, 64], P('dp', 'ctx')
- d_kv_latent: bfloat16 [4, 1024, 512], P('dp', 'ctx')
- d_key_rope: bfloat16 [4, 1024, 64], P('dp', 'ctx')
- grad_w_down: float32 [7168, 576], P(('dp', 'ctx'))
- grad_w_uv: float32 [512, 1024], P(('dp', 'ctx'))
Inputs may be any that keep to these rules, and one draw needn't show every extreme that they name: A permutation: blocks[k] is the position block of rows k * 64 to (k + 1) * 64 - 1 of every sequence.
All inputs are finite; a program needn't handle non-finite values.
Results may differ from a plain program's by a relative error of at most 0.028.
Values may be sent and summed in bfloat16 or wider, within the bound.
A program may use at most 128 MiB of HBM per device.

v0:
```python
import math

import jax
import jax.numpy as jnp
from jax import lax
from jax.sharding import PartitionSpec as P

softmax_scale = 1.0 / math.sqrt(192.0)


def reduce_values(value_part):
    return lax.psum_scatter(value_part, ("dp", "ctx"), scatter_dimension=0, tiled=True)


def body(layer_input, kv_latent, key_rope, q_latent, q_rope, saved_output, w_uv, d_out, blocks):
    wide = jnp.float32
    tokens = kv_latent.shape[1]
    half_rows = tokens // 2
    heads = q_latent.shape[2]
    latent = kv_latent.shape[2]
    rope_width = key_rope.shape[2]
    value_width = w_uv.shape[1] // heads
    block_count = blocks.shape[0]
    seq_rows = half_rows * block_count
    tile_rows = min(256, seq_rows)
    value_weight = w_uv.reshape(latent, heads, value_width)
    grad_out = d_out[0].reshape(tokens, heads, value_width)
    outputs = saved_output[0]
    value_part = jnp.einsum("thk,thv->khv", outputs, grad_out, preferred_element_type=wide).reshape(
        latent, heads * value_width
    )
    gathered_lat, gathered_rope = (
        lax.all_gather(kv_latent, "ctx", axis=1, tiled=True),
        lax.all_gather(key_rope, "ctx", axis=1, tiled=True),
    )
    block_ids = jnp.arange(block_count, dtype=jnp.int32)
    matches = blocks[None, :] == block_ids[:, None]
    source = jnp.sum(jnp.where(matches, block_ids[None, :], 0), axis=1)
    sorted_lat = jnp.take(
        gathered_lat[0].reshape(block_count, half_rows, latent), source, axis=0
    ).reshape(seq_rows, latent)
    sorted_rope = jnp.take(
        gathered_rope[0].reshape(block_count, half_rows, rope_width), source, axis=0
    ).reshape(seq_rows, rope_width)
    device_index = lax.axis_index("ctx")
    own_blocks = lax.dynamic_slice_in_dim(blocks, 2 * device_index, 2, 0)
    grad_lat = jnp.einsum(
        "thv,khv->thk", grad_out, value_weight, preferred_element_type=wide
    ).astype(jnp.bfloat16)
    row_count = half_rows * heads
    term_lat = jnp.zeros((seq_rows, latent), wide)
    term_rope = jnp.zeros((seq_rows, rope_width), wide)
    dq_parts = []
    for which in range(2):
        block_id = own_blocks[which]
        query_rows = q_latent[0, which * half_rows : (which + 1) * half_rows].reshape(
            row_count, latent
        )
        query_rope = q_rope[0, which * half_rows : (which + 1) * half_rows].reshape(
            row_count, rope_width
        )
        out_rows = outputs[which * half_rows : (which + 1) * half_rows].reshape(row_count, latent)
        grad_rows = grad_lat[which * half_rows : (which + 1) * half_rows].reshape(row_count, latent)
        query_pos = block_id * half_rows + jnp.arange(row_count, dtype=jnp.int32) // heads
        tile_count = ((block_id + 1) * half_rows + tile_rows - 1) // tile_rows

        def score_step(
            index_tile, buffer, query_rows=query_rows, query_rope=query_rope, query_pos=query_pos
        ):
            start = index_tile * tile_rows
            key_tile = lax.dynamic_slice_in_dim(sorted_lat, start, tile_rows, 0)
            rope_tile = lax.dynamic_slice_in_dim(sorted_rope, start, tile_rows, 0)
            scores = jnp.einsum("rk,jk->rj", query_rows, key_tile, preferred_element_type=wide)
            scores = scores + jnp.einsum(
                "rk,jk->rj", query_rope, rope_tile, preferred_element_type=wide
            )
            key_pos = start + jnp.arange(tile_rows, dtype=jnp.int32)
            visible = key_pos[None, :] <= query_pos[:, None]
            masked = jnp.where(visible, scores * softmax_scale, -jnp.inf)
            return lax.dynamic_update_slice_in_dim(buffer, masked, start, 1)

        buffer = lax.fori_loop(
            0, tile_count, score_step, jnp.full((row_count, seq_rows), -jnp.inf, wide)
        )
        row_max = jnp.max(buffer, axis=1)
        log_total = row_max + jnp.log(jnp.sum(jnp.exp(buffer - row_max[:, None]), axis=1))
        delta = jnp.sum(grad_rows.astype(wide) * out_rows.astype(wide), axis=1)

        def grad_step(
            index_tile,
            carry,
            query_rows=query_rows,
            query_rope=query_rope,
            buffer=buffer,
            log_total=log_total,
            grad_rows=grad_rows,
            delta=delta,
        ):
            dq_lat, dq_rope, acc_lat, acc_rope = carry
            start = index_tile * tile_rows
            key_tile = lax.dynamic_slice_in_dim(sorted_lat, start, tile_rows, 0)
            rope_tile = lax.dynamic_slice_in_dim(sorted_rope, start, tile_rows, 0)
            scores = lax.dynamic_slice_in_dim(buffer, start, tile_rows, 1)
            probs = jnp.exp(scores - log_total[:, None])
            probs_low = probs.astype(jnp.bfloat16)
            grad_prob = jnp.einsum("rk,jk->rj", grad_rows, key_tile, preferred_element_type=wide)
            grad_score = (probs * (grad_prob - delta[:, None])).astype(jnp.bfloat16)
            dq_lat = dq_lat + jnp.dot(grad_score, key_tile, preferred_element_type=wide)
            dq_rope = dq_rope + jnp.dot(grad_score, rope_tile, preferred_element_type=wide)
            key_lat = jnp.einsum("rj,rk->jk", probs_low, grad_rows, preferred_element_type=wide)
            key_lat = key_lat + softmax_scale * jnp.einsum(
                "rj,rk->jk", grad_score, query_rows, preferred_element_type=wide
            )
            key_rot = softmax_scale * jnp.einsum(
                "rj,rk->jk", grad_score, query_rope, preferred_element_type=wide
            )
            acc_lat = lax.dynamic_update_slice_in_dim(
                acc_lat, lax.dynamic_slice_in_dim(acc_lat, start, tile_rows, 0) + key_lat, start, 0
            )
            acc_rope = lax.dynamic_update_slice_in_dim(
                acc_rope,
                lax.dynamic_slice_in_dim(acc_rope, start, tile_rows, 0) + key_rot,
                start,
                0,
            )
            return (dq_lat, dq_rope, acc_lat, acc_rope)

        start_grads = (
            jnp.zeros((row_count, latent), wide),
            jnp.zeros((row_count, rope_width), wide),
            term_lat,
            term_rope,
        )
        dq_lat, dq_rope, term_lat, term_rope = lax.fori_loop(0, tile_count, grad_step, start_grads)
        dq_parts.append(
            (
                (softmax_scale * dq_lat).astype(jnp.bfloat16).reshape(half_rows, heads, latent),
                (softmax_scale * dq_rope)
                .astype(jnp.bfloat16)
                .reshape(half_rows, heads, rope_width),
            )
        )
    d_q_latent = jnp.concatenate([item[0] for item in dq_parts], axis=0)[None]
    d_q_rope = jnp.concatenate([item[1] for item in dq_parts], axis=0)[None]
    device_lat = jnp.take(
        term_lat.astype(jnp.bfloat16).reshape(block_count, half_rows, latent), blocks, axis=0
    ).reshape(1, seq_rows, latent)
    device_rope = jnp.take(
        term_rope.astype(jnp.bfloat16).reshape(block_count, half_rows, rope_width), blocks, axis=0
    ).reshape(1, seq_rows, rope_width)
    summed_lat, summed_rope = (
        lax.psum_scatter(device_lat, "ctx", scatter_dimension=1, tiled=True).astype(jnp.float32),
        lax.psum_scatter(device_rope, "ctx", scatter_dimension=1, tiled=True).astype(jnp.float32),
    )
    d_kv_latent = summed_lat.astype(jnp.bfloat16)
    d_key_rope = summed_rope.astype(jnp.bfloat16)
    joined = jnp.concatenate([d_kv_latent, d_key_rope], axis=2)
    down_part = jnp.einsum(
        "btd,btc->dc",
        layer_input,
        lax.all_gather(joined, "dp", axis=0, tiled=True),
        preferred_element_type=wide,
    )
    grad_down = lax.psum_scatter(
        down_part.astype(jnp.bfloat16), "ctx", scatter_dimension=0, tiled=True
    ).astype(jnp.float32)
    grad_uv = reduce_values(value_part)
    return (d_q_latent, d_q_rope, d_kv_latent, d_key_rope, grad_down, grad_uv)


def solution(mesh):
    in_specs = (
        P(None, "ctx", "dp"),
        P("dp", "ctx", None),
        P("dp", "ctx", None),
        P("dp", "ctx", None, None),
        P("dp", "ctx", None, None),
        P("dp", "ctx", None, None),
        P(),
        P("dp", "ctx", None),
        P(),
    )
    out_specs = (
        P("dp", "ctx", None, None),
        P("dp", "ctx", None, None),
        P("dp", "ctx", None),
        P("dp", "ctx", None),
        P(("dp", "ctx"), None),
        P(("dp", "ctx"), None),
    )
    return jax.shard_map(body, mesh=mesh, in_specs=in_specs, out_specs=out_specs, check_vma=False)
```

profile of v0, /device:TPU:27, one launch (start us, length us, event | category | flops | bytes accessed | tf_op | source)
XLA Modules:
  0.0 412.6 jit_solution(17377967121509350652)
XLA Ops:
  10.1 1.1 copy.103
  11.2 1.8 fusion.82
  13.1 1.3 fusion.81
  15.4 12.9 %all_gather.10 = bf16[1,1024,64]{1,2,0:T(8,128)(2,1)S(1)} all-gather(bf16[1,128,64]{1,2,0:T(8,128)(2,1)S(1)} %copy-done.18), channel_id=1, replica_groups=mesh['dp'=4,'ctx'=8] {'ctx'}, dimensions={1}, use_global_device_ids=true | all-gather | bytes 147456 | tf_op jit(solution)/shard_map/all_gather | solution.py:34
  35.2 1.2 compare_and_fusion
  38.9 1.5 copy_bitcast_fusion.5
  40.5 2.8 gather_fusion
  43.3 1.4 broadcast_select_fusion.1
  44.7 1.6 broadcast.95.clone
  46.2 3.4 while.56
  46.3 1.4 fusion.191
  47.6 2.0 fusion.193
  49.6 1.8 reduce_max.18
  51.4 1.9 exponential_reduce_fusion.1
  54.8 1.1 broadcast.93.clone
  55.9 1.6 broadcast_in_dim.62
  57.5 9.5 %while.54 = (s32[]{:T(128)}, f32[512,512]{1,0:T(8,128)}, f32[512,64]{0,1:T(8,128)}, f32[1024,512]{1,0:T(8,128)}, f32[1024,64]{0,1:T(8,128)}, /*index=5*/s32[]{:T...) while((s32[]{:T(128)}, f32[512,512]{1,0:T(8,128)}, ...), condition=%wide.region_7.10_spmd, body=%wide.region_6.9_spmd.sunk | while | flops 571932672 | bytes 22027636 | solution.py:134
  57.5 1.7 fusion.167
  59.1 1.8 convolution_add_fusion.11
  61.0 1.7 fusion.170
  62.6 1.4 fusion.168
  64.4 2.5 fusion.169
  67.0 1.6 broadcast.95.clone.1
  68.6 6.7 %while.57 = (s32[]{:T(128)}, f32[512,1024]{0,1:T(8,128)}, s32[]{:T(128)}, bf16[1024,512]{1,0:T(8,128)(2,1)S(1)}, bf16[512,512]{1,0:T(8,128)(2,1)S(1)}, /*index=5...) while((s32[]{:T(128)}, f32[512,1024]{0,1:T(8,128)}, ...), condition=%wide.region_9.12_spmd.clone, body=%wide.region_8.11_spmd.clone.sunk | while | flops 151524096 | bytes 2497711 | solution.py:82
  68.9 1.9 fusion.200
  71.1 1.9 fusion.200
  73.3 1.9 fusion.200
  75.2 1.8 reduce_max.19
  77.0 1.9 exponential_reduce_fusion
  79.7 1.1 broadcast.93
  80.8 28.3 %while.55 = (s32[]{:T(128)}, f32[512,512]{1,0:T(8,128)}, f32[512,64]{0,1:T(8,128)}, f32[1024,512]{1,0:T(8,128)}, f32[1024,64]{0,1:T(8,128)}, /*index=5*/s32[]{:T...) while((s32[]{:T(128)}, f32[512,512]{1,0:T(8,128)}, ...), condition=%wide.region_14.17_spmd, body=%wide.region_13.16_spmd.sunk | while | flops 571932672 | bytes 19668284 | solution.py:134
  80.8 1.6 fusion.183
  82.4 1.8 convolution_add_fusion.13
  84.2 1.7 fusion.186
  85.9 1.3 fusion.184
  87.6 2.5 fusion.185
  90.2 1.7 fusion.183
  91.8 1.8 convolution_add_fusion.13
  93.7 1.7 fusion.186
  95.3 1.3 fusion.184
  97.1 2.5 fusion.185
  99.6 1.7 fusion.183
  101.3 1.8 convolution_add_fusion.13
  103.1 1.7 fusion.186
  104.8 1.3 fusion.184
  106.5 2.6 fusion.185
  112.3 1.7 convert_element_type.83
  114.0 1.7 gather_fusion.2
  115.7 1.4 broadcast_select_fusion
  117.1 1.6 copy.123
  118.8 1.3 copy.124
  120.1 59.9 %reduce-scatter.15.cloned.1.call-done = bf16[128,64]{1,0:T(8,128)(2,1)} async-done(((bf16[1024,64]{1,0:T(8,128)(2,1)}), bf16[128,64]{1,0:T(8,128)(2,1)}) %reduce-scatter.15.cloned.1.call-update) | async-done | bytes 16400
  180.9 32.3 %reduce-scatter.13.cloned.1.call-done = bf16[128,512]{1,0:T(8,128)(2,1)} async-done(((bf16[1024,512]{1,0:T(8,128)(2,1)}), bf16[128,512]{1,0:T(8,128)(2,1)}) %reduce-scatter.13.cloned.1.call-update) | async-done | bytes 131088
  214.5 10.2 %all_gather.11 = bf16[4,128,576]{1,2,0:T(8,128)(2,1)S(1)} all-gather(bf16[1,128,576]{1,2,0:T(8,128)(2,1)S(1)} %pad_maximum_fusion), channel_id=1, replica_groups=mesh['dp'=4,'ctx'=8] {'dp'}, dimensions={0}, use_global_device_ids=true | all-gather | bytes 737280 | tf_op jit(solution)/shard_map/all_gather | solution.py:161
  224.7 2.5 fusion.68
  227.2 4.1 copy.94
  231.4 1.1 copy-done.12
  232.6 2.2 fusion.74
  234.8 2.9 copy.86
  243.1 1.4 fusion.76
  244.6 1.1 maximum_bitcast_fusion
  246.4 20.8 %reduce-scatter.17.cloned.1.call-done = bf16[224,576]{1,0:T(8,128)(2,1)} async-done(((bf16[1792,576]{1,0:T(8,128)(2,1)}), bf16[224,576]{1,0:T(8,128)(2,1)}) %reduce-scatter.17.cloned.1.call-update) | async-done | bytes 258064
  267.1 1.1 copy.95
  269.2 136.8 %reduce-scatter.11.cloned.1.call-done = f32[16,1024]{1,0:T(8,128)} async-done(((f32[512,1024]{1,0:T(8,128)}), f32[16,1024]{1,0:T(8,128)}) %reduce-scatter.11.cloned.1.call-update) | async-done | bytes 65552 | tf_op jit(solution)/shard_map/reduce_scatter | solution.py:12
  (125 shorter events, 27.8 us)
Async XLA Ops:
  7.2 217.5 %copy-start = (bf16[4,128,1792]{2,1,0:T(8,128)(2,1)S(1)}, bf16[4,128,1792]{2,1,0:T(8,128)(2,1)}, u32[]{:S(2)}) copy-start(bf16[4,128,1792]{2,1,0:T(8,128)(2,1)} %param.21) | copy-start | bytes 5505028
  7.2 33.3 %all-gather.2.cloned.1.call-start = ((), (), s32[]{:S(2)}) async-start(), calls=%async_computation.4 | async-start | bytes 1179648 | tf_op jit(solution)/shard_map/all_gather | solution.py:33
  7.9 172.1 %reduce-scatter.15.cloned.1.call-start = ((), (), s32[]{:S(2)}) async-start(), calls=%async_computation.7 | async-start | bytes 294912
  8.7 5.6 %copy-start.20 = (s32[16]{0:T(128)}, s32[16]{0:T(128)S(1)}, u32[]{:S(2)}) copy-start(s32[16]{0:T(128)S(1)} %select_reduce_fusion) | copy-start | bytes 196
  11.2 3.7 copy-start.13
  11.2 3.1 copy-start.15
  14.4 1.1 copy-start.18
  33.9 4.2 %copy-start.16 = (bf16[1,128,8,512]{3,2,1,0:T(8,128)(2,1)S(1)}, bf16[1,128,8,512]{3,2,1,0:T(8,128)(2,1)}, u32[]{:S(2)}) copy-start(bf16[1,128,8,512]{3,2,1,0:T(8,128)(2,1)} %param.24) | copy-start | bytes 3145732
  57.5 3.5 copy-start.9
  57.5 5.2 %copy-start.3 = (bf16[512,512]{1,0:T(8,128)(2,1)S(1)}, bf16[512,512]{1,0:T(8,128)(2,1)}, u32[]{:S(2)}) copy-start(bf16[512,512]{1,0:T(8,128)(2,1)} %get-tuple-element.775) | copy-start | bytes 1572868 | tf_op jit(solution)/shard_map/while
  57.5 6.6 %copy-start.7 = (f32[512,512]{1,0:T(8,128)S(1)}, f32[512,512]{1,0:T(8,128)}, u32[]{:S(2)}) copy-start(f32[512,512]{1,0:T(8,128)} %get-tuple-element.749) | copy-start | bytes 3145732 | tf_op jit(solution)/shard_map/while
  62.6 1.8 copy-start.1
  64.4 2.5 copy-start.8
  80.8 30.2 %copy-start.19 = (pred[16]{0:T(512)(128)(4,1)S(1)}, pred[16]{0:T(512)(128)(4,1)}, u32[]{:S(2)}) copy-start(pred[16]{0:T(512)(128)(4,1)} %compare_and_fusion) | copy-start | bytes 52
  80.8 5.2 %copy-start.2 = (bf16[512,512]{1,0:T(8,128)(2,1)S(1)}, bf16[512,512]{1,0:T(8,128)(2,1)}, u32[]{:S(2)}) copy-start(bf16[512,512]{1,0:T(8,128)(2,1)} %get-tuple-element.865) | copy-start | bytes 1572868 | tf_op jit(solution)/shard_map/while
  80.8 6.5 %copy-start.4 = (f32[512,512]{1,0:T(8,128)S(1)}, f32[512,512]{1,0:T(8,128)}, u32[]{:S(2)}) copy-start(f32[512,512]{1,0:T(8,128)} %get-tuple-element.839) | copy-start | bytes 3145732 | tf_op jit(solution)/shard_map/while
  87.6 2.5 copy-start.5
  90.2 5.2 %copy-start.2 = (bf16[512,512]{1,0:T(8,128)(2,1)S(1)}, bf16[512,512]{1,0:T(8,128)(2,1)}, u32[]{:S(2)}) copy-start(bf16[512,512]{1,0:T(8,128)(2,1)} %get-tuple-element.865) | copy-start | bytes 1572868 | tf_op jit(solution)/shard_map/while
  90.2 6.5 %copy-start.4 = (f32[512,512]{1,0:T(8,128)S(1)}, f32[512,512]{1,0:T(8,128)}, u32[]{:S(2)}) copy-start(f32[512,512]{1,0:T(8,128)} %get-tuple-element.839) | copy-start | bytes 3145732 | tf_op jit(solution)/shard_map/while
  97.1 2.6 copy-start.5
  99.6 5.2 %copy-start.2 = (bf16[512,512]{1,0:T(8,128)(2,1)S(1)}, bf16[512,512]{1,0:T(8,128)(2,1)}, u32[]{:S(2)}) copy-start(bf16[512,512]{1,0:T(8,128)(2,1)} %get-tuple-element.865) | copy-start | bytes 1572868 | tf_op jit(solution)/shard_map/while
  99.6 6.5 %copy-start.4 = (f32[512,512]{1,0:T(8,128)S(1)}, f32[512,512]{1,0:T(8,128)}, u32[]{:S(2)}) copy-start(f32[512,512]{1,0:T(8,128)} %get-tuple-element.839) | copy-start | bytes 3145732 | tf_op jit(solution)/shard_map/while
  106.5 2.6 copy-start.5
  112.2 101.0 %reduce-scatter.13.cloned.1.call-start = ((), (), s32[]{:S(2)}) async-start(), calls=%async_computation.6 | async-start | bytes 1179648
  120.0 147.1 %reduce-scatter.17.cloned.1.call-start = ((), (), s32[]{:S(2)}) async-start(), calls=%async_computation.8 | async-start | bytes 2580480
  180.9 46.3 %copy-start.17 = (bf16[1,128,64]{1,2,0:T(8,128)(2,1)}, bf16[1,128,64]{1,2,0:T(8,128)(2,1)S(1)}, u32[]{:S(2)}) copy-start(bf16[1,128,64]{1,2,0:T(8,128)(2,1)S(1)} %copy.93) | copy-start | bytes 49156
  231.3 1.2 copy-start.12
  231.3 1.3 copy-start.14
  231.4 174.7 %reduce-scatter.11.cloned.1.call-start = ((), (), s32[]{:S(2)}) async-start(), calls=%async_computation.5 | async-start | bytes 2162688 | tf_op jit(solution)/shard_map/reduce_scatter | solution.py:12
  237.6 0.9 copy-start.11
  237.6 1.8 copy-start.10
  237.7 6.8 %copy-start.6 = (f32[512,512]{1,0:T(8,128)S(1)}, f32[512,512]{1,0:T(8,128)}, u32[]{:S(2)}) copy-start(f32[512,512]{1,0:T(8,128)} %get-tuple-element.251) | copy-start | bytes 3145732
Sparse Core Ops, SparseCore 0:
  9.6 22.9 all-gather.1
  112.4 67.6 reduce-scatter.14
  182.3 30.9 reduce-scatter.12
  231.5 35.6 reduce-scatter.16
  269.8 136.1 reduce-scatter.10
where the time goes:
time: 418 us; the launch traced here: 413 us
  waiting for transfers between devices  251 us (60%)
  matrix products  52.8 us (13%)
  local copies, waits for them, and re-layouts  46 us (11%)
  other arithmetic  23 us (6%)
  blocking collectives  23 us (6%)
  between operations  16.7 us (4%)
    reduce_scatter x1, waiting for transfers between devices, reduce_values(): lax.psum_scatter(value_part, ('dp', 'ctx'), scatter_dimension=0, tiled=True)  137 us
    unnamed x8, waiting for transfers between devices  114 us
    unnamed x39, local copies, waits for them, and re-layouts  16 us
    all_gather x1, blocking collectives, body(): lax.all_gather(key_rope, 'ctx', axis=1, tiled=True)  12.9 us
    dot_general x4, matrix products, grad_step(): jnp.einsum('rj,rk->jk', grad_score, query_rows, preferred_element_type=wide)  10.2 us
    all_gather x1, blocking collectives, body(): lax.all_gather(joined, 'dp', axis=0, tiled=True)  10.2 us
  transfers between devices with their start and end apart: 5, of which 4 were waited for; matrix products, arithmetic and copies ran while one was open for 10% of the time, Pallas kernels for 0%

commit v1 on v0

v1 whole, which is shorter than its diff:
```python
import functools
import math

import jax
import jax.numpy as jnp
from jax import lax
from jax.experimental import pallas as pl
from jax.experimental.pallas import tpu as pltpu
from jax.sharding import PartitionSpec as P

softmax_scale = 1.0 / math.sqrt(192.0)
wide = jnp.float32
low = jnp.bfloat16
MESH = pl.DeviceIdType.MESH
VMEM_LIMIT = 62 * 1024 * 1024


def dot(a, b, ca, cb):
    return lax.dot_general(a, b, (((ca,), (cb,)), ((), ())), preferred_element_type=wide)


def greet(peers):
    barrier = pltpu.get_barrier_semaphore()
    for peer in peers:
        pl.semaphore_signal(barrier, inc=1, device_id=peer, device_id_type=MESH)
    pl.semaphore_wait(barrier, len(peers))


def remote(src, dst, send, recv, peer):
    return pltpu.make_async_remote_copy(
        src_ref=src, dst_ref=dst, send_sem=send, recv_sem=recv, device_id=peer, device_id_type=MESH
    )


def gather_kernel(
    n_dp, n_ctx,
    key_ref, spread_ref, weight_ref, saved_ref,
    keys_ref, grad_ref, delta_ref, value_ref,
    parts, landed, key_send, key_recv, pair_send, pair_recv, val_send, val_recv,
):
    dp, ctx = lax.axis_index("dp"), lax.axis_index("ctx")
    n_z = n_ctx // 2
    z, core = ctx // 2, ctx % 2
    tokens = key_ref.shape[0]
    partner = (dp, z * 2 + (1 - core))
    z_peer = lambda k: (dp, lax.rem(z + k, n_z) * 2 + core)
    dp_peer = lambda k: (lax.rem(dp + k, n_dp), ctx)
    greet(
        [partner]
        + [z_peer(k) for k in range(1, n_z)]
        + [dp_peer(k) for k in range(1, n_dp)]
    )

    def rows_of(index):
        return keys_ref.at[pl.ds(pl.multiple_of(index * tokens, tokens), tokens)]

    sends = []
    for k in range(1, n_z):
        copy = remote(key_ref, rows_of(ctx), key_send.at[k], key_recv.at[k], z_peer(k))
        copy.start()
        sends.append(copy)
    pair = remote(key_ref, rows_of(ctx), pair_send.at[0], pair_recv.at[0], partner)
    pair.start()
    keys_ref[pl.ds(pl.multiple_of(ctx * tokens, tokens), tokens), :] = key_ref[...]

    share = parts.shape[1]
    value = dot(saved_ref[...], spread_ref[...], 0, 0).astype(low)
    for d in range(n_dp):
        parts[d] = value[d * share : (d + 1) * share]
    value_copies = []
    for k in range(1, n_dp):
        copy = remote(
            parts.at[lax.rem(dp + k, n_dp)], landed.at[k], val_send.at[k], val_recv.at[k], dp_peer(k)
        )
        copy.start()
        value_copies.append(copy)

    rows = spread_ref.shape[0]
    tile = min(256, rows)
    for start in range(0, rows, tile):
        grad = dot(spread_ref[start : start + tile], weight_ref[...], 1, 1).astype(low)
        grad_ref[start : start + tile, :] = grad
        prod = grad.astype(wide) * saved_ref[start : start + tile].astype(wide)
        part = prod[:, :128]
        for lane in range(128, prod.shape[1], 128):
            part = part + prod[:, lane : lane + 128]
        delta_ref[:, start : start + tile] = jnp.sum(part.T, axis=0, keepdims=True)

    passes = []
    for k in range(1, n_z):
        owner = lax.rem(z + n_z - k, n_z) * 2 + core
        remote(key_ref, rows_of(owner), key_send.at[k], key_recv.at[k], z_peer(k)).wait_recv()
        copy = remote(rows_of(owner), rows_of(owner), pair_send.at[k], pair_recv.at[k], partner)
        copy.start()
        passes.append(copy)
    total = parts[dp].astype(wide)
    for k in range(1, n_dp):
        value_copies[k - 1].wait_recv()
        total = total + landed[k].astype(wide)
    total = total.astype(low)
    piece = value_ref.shape[1]
    for c in range(n_ctx):
        value_ref[c] = total[c * piece : (c + 1) * piece]
    for k in range(n_z):
        owner = lax.rem(z + n_z - k, n_z) * 2 + (1 - core)
        remote(rows_of(owner), rows_of(owner), pair_send.at[k], pair_recv.at[k], partner).wait_recv()
    for copy in sends + [pair] + passes + value_copies:
        copy.wait_send()


def attend_kernel(
    keys_ref, posk_ref, posq_ref, delta_ref, ql_ref, qr_ref, grad_ref,
    dql_ref, dqr_ref, term_ref, total,
):
    step = pl.program_id(0)
    latent = ql_ref.shape[1]
    key_lat = keys_ref[:, :latent]
    key_rope = keys_ref[:, latent:]
    ql, qr, grad = ql_ref[...], qr_ref[...], grad_ref[...]
    scores = (dot(key_lat, ql, 1, 1) + dot(key_rope, qr, 1, 1)) * softmax_scale
    scores = jnp.where(posk_ref[...] <= posq_ref[...], scores, -jnp.inf)
    top = jnp.max(scores, axis=0, keepdims=True)
    expo = jnp.exp(scores - top)
    probs = expo * (1.0 / jnp.sum(expo, axis=0, keepdims=True))
    grad_prob = dot(key_lat, grad, 1, 1)
    slope = (probs * (grad_prob - delta_ref[...])).astype(low)
    dql_ref[...] = (softmax_scale * dot(slope, key_lat, 0, 0)).astype(low)
    dqr_ref[...] = (softmax_scale * dot(slope, key_rope, 0, 0)).astype(low)
    lat = dot(probs.astype(low), grad, 1, 0) + softmax_scale * dot(slope, ql, 1, 0)
    rope = softmax_scale * dot(slope, qr, 1, 0)

    @pl.when(step == 0)
    def _():
        total[:, :latent] = lat
        total[:, latent:] = rope

    @pl.when(step > 0)
    def _():
        total[:, :latent] += lat
        total[:, latent:] += rope

    @pl.when(step == pl.num_programs(0) - 1)
    def _():
        term_ref[...] = total[...].astype(low)


def reduce_kernel(
    n_dp, n_ctx,
    term_ref, layer_ref, value_ref,
    joined_ref, down_ref, uv_ref,
    turned, pair_in, pair_sum, z_in, blocks_in, down_out, down_own, down_in, down_sum, down_z, value_in,
    a_send, a_recv, b_send, b_recv, c_send, c_recv, d_send, d_recv, e_send, e_recv, f_send, f_recv,
):
    dp, ctx = lax.axis_index("dp"), lax.axis_index("ctx")
    n_z = n_ctx // 2
    z, core = ctx // 2, ctx % 2
    tokens = joined_ref.shape[0]
    other = 1 - core
    partner = (dp, z * 2 + other)
    chip = lambda k: lax.rem(z + k, n_z)
    z_peer = lambda k: (dp, chip(k) * 2 + core)
    dp_peer = lambda k: (lax.rem(dp + k, n_dp), ctx)
    ctx_peer = lambda k: (dp, lax.rem(ctx + k, n_ctx))
    greet([ctx_peer(k) for k in range(1, n_ctx)] + [dp_peer(k) for k in range(1, n_dp)])
    order = list(range(1, n_z)) + [0]
    pending = []

    def send(src, dst, s, r, peer):
        copy = remote(src, dst, s, r, peer)
        copy.start()
        pending.append(copy)
        return copy

    def term_rows(index):
        return pl.ds(pl.multiple_of(index * tokens, tokens), tokens)

    first = {}
    for k in order:
        first[k] = send(
            term_ref.at[term_rows(chip(k) * 2 + other)], pair_in.at[k], a_send.at[k], a_recv.at[k], partner
        )
    second = {}
    mine = None
    for k in order:
        first[k].wait_recv()
        added = term_ref[term_rows(chip(k) * 2 + core), :].astype(wide) + pair_in[k].astype(wide)
        if k == 0:
            mine = added
        else:
            pair_sum[k] = added.astype(low)
            second[k] = send(pair_sum.at[k], z_in.at[k], b_send.at[k], b_recv.at[k], z_peer(k))
    batch = layer_ref.shape[0]
    for d in range(batch):
        turned[:, d * tokens : (d + 1) * tokens] = layer_ref[d].T
    for k in range(1, n_z):
        second[k].wait_recv()
        mine = mine + z_in[k].astype(wide)
    joined_ref[...] = mine.astype(low)
    blocks_in[dp] = mine.astype(low)

    third = []
    for k in range(1, n_dp):
        third.append(send(joined_ref, blocks_in.at[dp], c_send.at[k], c_recv.at[k], dp_peer(k)))
    values = []
    for k in range(1, n_ctx):
        values.append(
            send(
                value_ref.at[lax.rem(ctx + k, n_ctx)], value_in.at[k], d_send.at[k], d_recv.at[k], ctx_peer(k)
            )
        )
    for copy in third:
        copy.wait_recv()
    every = blocks_in[...].reshape(batch * tokens, blocks_in.shape[2])

    height = down_ref.shape[0]

    def turned_rows(index):
        return turned[pl.ds(pl.multiple_of(index * height, 16), height), :]

    fourth = {}
    for k in order:
        down_out[k] = dot(turned_rows(chip(k) * 2 + other), every, 1, 0).astype(low)
        fourth[k] = send(down_out.at[k], down_in.at[k], e_send.at[k], e_recv.at[k], partner)
    fifth = {}
    own = None
    for k in order:
        part = dot(turned_rows(chip(k) * 2 + core), every, 1, 0)
        fourth[k].wait_recv()
        part = part + down_in[k].astype(wide)
        if k == 0:
            down_own[...] = part
        else:
            down_sum[k] = part.astype(low)
            fifth[k] = send(down_sum.at[k], down_z.at[k], f_send.at[k], f_recv.at[k], z_peer(k))
    value = value_ref[ctx].astype(wide)
    for k in range(1, n_ctx):
        values[k - 1].wait_recv()
        value = value + value_in[k].astype(wide)
    uv_ref[...] = value
    for k in range(1, n_z):
        fifth[k].wait_recv()
        down_own[...] += down_z[k].astype(wide)
    down_ref[...] = down_own[...]
    for copy in pending:
        copy.wait_send()


def body(n_dp, n_ctx, layer_input, kv_latent, key_rope, q_latent, q_rope, saved_output, w_uv, d_out, blocks):
    tokens = kv_latent.shape[1]
    half_rows = tokens // 2
    heads, latent = q_latent.shape[2], q_latent.shape[3]
    rope_width = key_rope.shape[2]
    width = latent + rope_width
    value_width = w_uv.shape[1] // heads
    seq_rows = half_rows * blocks.shape[0]
    rows = tokens * heads
    n_z = n_ctx // 2
    values = w_uv.shape[1]
    vmem = pl.BlockSpec(memory_space=pltpu.VMEM)
    dma = lambda n: pltpu.SemaphoreType.DMA((n,))

    keys = jnp.concatenate([kv_latent[0], key_rope[0]], axis=1)
    head_of = jnp.arange(values, dtype=jnp.int32) // value_width
    keep = head_of[None, :] == jnp.arange(heads, dtype=jnp.int32)[:, None]
    spread = jnp.where(keep[None], d_out[0][:, None, :], jnp.zeros((), low)).reshape(rows, values)
    saved = saved_output[0].reshape(rows, latent)
    offsets = jnp.arange(half_rows, dtype=jnp.int32)
    pos_key = (blocks[:, None] * half_rows + offsets[None, :]).reshape(seq_rows, 1)
    own_blocks = lax.dynamic_slice_in_dim(blocks, 2 * lax.axis_index("ctx"), 2, 0)
    pos_query = jnp.repeat(
        (own_blocks[:, None] * half_rows + offsets[None, :]).reshape(tokens), heads
    ).reshape(1, rows)

    all_keys, grad, delta, value_sum = pl.pallas_call(
        functools.partial(gather_kernel, n_dp, n_ctx),
        out_shape=(
            jax.ShapeDtypeStruct((seq_rows, width), low),
            jax.ShapeDtypeStruct((rows, latent), low),
            jax.ShapeDtypeStruct((1, rows), wide),
            jax.ShapeDtypeStruct((n_ctx, latent // (n_dp * n_ctx), values), low),
        ),
        in_specs=[vmem] * 4,
        out_specs=(vmem,) * 4,
        scratch_shapes=[
            pltpu.VMEM((n_dp, latent // n_dp, values), low),
            pltpu.VMEM((n_dp, latent // n_dp, values), low),
            dma(n_z), dma(n_z), dma(n_z), dma(n_z), dma(n_dp), dma(n_dp),
        ],
        compiler_params=pltpu.CompilerParams(
            collective_id=0, has_side_effects=True, vmem_limit_bytes=VMEM_LIMIT
        ),
        name="gather",
    )(keys, spread, w_uv, saved)

    tile = min(256, rows)
    whole = lambda shape: pl.BlockSpec(shape, lambda i: (0, 0))
    d_lat, d_rope, term = pl.pallas_call(
        attend_kernel,
        grid=(rows // tile,),
        out_shape=(
            jax.ShapeDtypeStruct((rows, latent), low),
            jax.ShapeDtypeStruct((rows, rope_width), low),
            jax.ShapeDtypeStruct((seq_rows, width), low),
        ),
        in_specs=[
            whole((seq_rows, width)),
            whole((seq_rows, 1)),
            pl.BlockSpec((1, tile), lambda i: (0, i)),
            pl.BlockSpec((1, tile), lambda i: (0, i)),
            pl.BlockSpec((tile, latent), lambda i: (i, 0)),
            pl.BlockSpec((tile, rope_width), lambda i: (i, 0)),
            pl.BlockSpec((tile, latent), lambda i: (i, 0)),
        ],
        out_specs=(
            pl.BlockSpec((tile, latent), lambda i: (i, 0)),
            pl.BlockSpec((tile, rope_width), lambda i: (i, 0)),
            whole((seq_rows, width)),
        ),
        scratch_shapes=[pltpu.VMEM((seq_rows, width), wide)],
        compiler_params=pltpu.CompilerParams(
            dimension_semantics=("arbitrary",), vmem_limit_bytes=VMEM_LIMIT
        ),
        name="attend",
    )(
        all_keys, pos_key, pos_query, delta,
        q_latent[0].reshape(rows, latent), q_rope[0].reshape(rows, rope_width), grad,
    )

    height = layer_input.shape[2] // n_ctx
    batch = layer_input.shape[0]
    joined, grad_down, grad_uv = pl.pallas_call(
        functools.partial(reduce_kernel, n_dp, n_ctx),
        out_shape=(
            jax.ShapeDtypeStruct((tokens, width), low),
            jax.ShapeDtypeStruct((height, width), wide),
            jax.ShapeDtypeStruct((latent // (n_dp * n_ctx), values), wide),
        ),
        in_specs=[vmem] * 3,
        out_specs=(vmem,) * 3,
        scratch_shapes=[
            pltpu.VMEM((layer_input.shape[2], batch * tokens), low),
            pltpu.VMEM((n_z, tokens, width), low),
            pltpu.VMEM((n_z, tokens, width), low),
            pltpu.VMEM((n_z, tokens, width), low),
            pltpu.VMEM((n_dp, tokens, width), low),
            pltpu.VMEM((n_z, height, width), low),
            pltpu.VMEM((height, width), wide),
            pltpu.VMEM((n_z, height, width), low),
            pltpu.VMEM((n_z, height, width), low),
            pltpu.VMEM((n_z, height, width), low),
            pltpu.VMEM((n_ctx, latent // (n_dp * n_ctx), values), low),
            dma(n_z), dma(n_z), dma(n_z), dma(n_z), dma(n_dp), dma(n_dp),
            dma(n_ctx), dma(n_ctx), dma(n_z), dma(n_z), dma(n_z), dma(n_z),
        ],
        compiler_params=pltpu.CompilerParams(
            collective_id=1, has_side_effects=True, vmem_limit_bytes=VMEM_LIMIT
        ),
        name="reduce",
    )(term, layer_input, value_sum)
    return (
        d_lat.reshape(1, tokens, heads, latent),
        d_rope.reshape(1, tokens, heads, rope_width),
        joined[None, :, :latent],
        joined[None, :, latent:],
        grad_down,
        grad_uv,
    )


def solution(mesh):
    n_dp, n_ctx = mesh.shape["dp"], mesh.shape["ctx"]
    in_specs = (
        P(None, "ctx", "dp"),
        P("dp", "ctx", None),
        P("dp", "ctx", None),
        P("dp", "ctx", None, None),
        P("dp", "ctx", None, None),
        P("dp", "ctx", None, None),
        P(),
        P("dp", "ctx", None),
        P(),
    )
    out_specs = (
        P("dp", "ctx", None, None),
        P("dp", "ctx", None, None),
        P("dp", "ctx", None),
        P("dp", "ctx", None),
        P(("dp", "ctx"), None),
        P(("dp", "ctx"), None),
    )
    return jax.shard_map(
        functools.partial(body, n_dp, n_ctx),
        mesh=mesh, in_specs=in_specs, out_specs=out_specs, check_vma=False,
    )
```

time: 418 us -> 117 us (0.28); the launches traced: 413 us -> 117 us
  waiting for transfers between devices: 251 us -> 0 us
  Pallas kernels: 0 us -> 97.4 us
  matrix products: 52.8 us -> 0 us
  local copies, waits for them, and re-layouts: 46 us -> 12.9 us
  blocking collectives: 23 us -> 0 us
  other arithmetic: 23 us -> 5.69 us
  between operations: 16.7 us -> 0.67 us
    reduce_scatter x1 -> x0, waiting for transfers between devices: 137 us -> none  [reduce_values(): lax.psum_scatter(value_part, ('dp', 'ctx'), scatter_dimension=0, tiled=True)]
    unnamed x8 -> x0, waiting for transfers between devices: 114 us -> none
    pallas_call x0 -> x3, Pallas kernels: none -> 97.4 us  [the longest x1 60.3 us: body(): pl.pallas_call(functools.partial(reduce_kernel, n_dp, n_ctx), out_shape=(...]
    dot_general x35 -> x0, matrix products: 52.8 us -> none  [the longest x4 10.2 us: grad_step(): jnp.einsum('rj,rk->jk', grad_score, query_rows, preferred_element_type=wide)]
    all_gather x2 -> x0, blocking collectives: 23 us -> none  [the longest x1 12.9 us: body(): lax.all_gather(key_rope, 'ctx', axis=1, tiled=True)]
    another operation x8 -> x1, local copies, waits for them, and re-layouts: 8.68 us -> 0.71 us  [body(): pos_query = jnp.repeat((own_blocks[:, None] * half_rows + offsets[None, :...]
    unnamed x39 -> x6, local copies, waits for them, and re-layouts: 16 us -> 8.43 us
    gather x4 -> x0, local copies, waits for them, and re-layouts: 5.85 us -> none  [the longest x1 2.81 us: body(): jnp.take(gathered_lat[0].reshape(block_count, half_rows, latent), source,...]
  transfers between devices with their start and end apart: 5 -> 0, of which waited for: 4 -> 0; matrix products, arithmetic and copies ran while one was open for 10% -> 0% of each run, Pallas kernels for 0% -> 0%
where the time goes in v1:
time: 117 us
  Pallas kernels  97.4 us (83%)
  local copies, waits for them, and re-layouts  12.9 us (11%)
  other arithmetic  5.69 us (5%)
    pallas_call x1, Pallas kernels, body(): pl.pallas_call(functools.partial(reduce_kernel, n_dp, n_ctx), out_shape=(...  60.3 us
    pallas_call x1, Pallas kernels, body(): pl.pallas_call(functools.partial(gather_kernel, n_dp, n_ctx), out_shape=(...  23.1 us
    pallas_call x1, Pallas kernels, body(): pl.pallas_call(attend_kernel, grid=(rows // tile,), out_shape=(jax.ShapeD...  14.1 us
    unnamed x6, local copies, waits for them, and re-layouts  8.43 us
    select_n x1, other arithmetic, body(): jnp.where(keep[None], d_out[0][:, None, :], jnp.zeros((), low))  2.56 us

profile of v1, /device:TPU:27, one launch (start us, length us, event | category | flops | bytes accessed | tf_op | source)
XLA Modules:
  0.0 116.7 jit_solution(9679015410943341743)
XLA Ops:
  0.6 0.7 dynamic-slice_multiply_fusion
  1.4 0.1 iota_add_fusion.1
  1.4 0.1 add.56
  1.5 0.7 broadcast_multiply_fusion
  2.2 0.1 iota_add_fusion
  2.3 0.8 copy.19
  3.1 0.1 broadcast_in_dim.42
  3.2 0.7 reshape_reshape.3.posq_ref
  3.9 1.6 %pad_maximum_fusion.key_ref = bf16[128,576]{1,0:T(8,128)(2,1)} fusion(bf16[128,64]{1,0:T(8,128)(2,1)S(1)} %bitcast.19, bf16[128,512]{1,0:T(8,128)(2,1)} %bitcast.20), kind=kLoop, calls=%fused_computation.1 | loop fusion | flops 294912 | bytes 294912 | tf_op jit(solution)/shard_map/concatenate | solution.py:262
  5.5 1.8 %copy.20 = bf16[1,128,8,64]{3,2,1,0:T(8,128)(2,1)} copy(bf16[1,128,8,64]{1,3,2,0:T(8,128)(2,1)} %param.13) | data formatting | bytes 262144 | tf_op args[4]
  7.2 1.3 %add.57.posk_ref = s32[1024,1]{1,0:T(8,128)} reshape(s32[16,64]{1,0:T(8,128)S(1)} %iota_add_fusion) | data formatting | bytes 8192 | tf_op jit(solution)/shard_map/add | solution.py:268
  8.5 2.6 %select_bitcast_fusion.spread_ref = bf16[1024,1024]{1,0:T(8,128)(2,1)} fusion(pred[8,1024]{1,0:T(8,128)(4,1)S(1)} %iota_compare_fusion, bf16[128,1024]{1,0:T(8,128)(2,1)} %bitcast.17), kind=kLoop, calls=%fused_computation | loop fusion | flops 1048576 | bytes 2367488 | tf_op jit(solution)/shard_map/jit(_where)/select_n | solution.py:265
  11.1 23.1 %gather.1 = (bf16[1024,576]{1,0:T(8,128)(2,1)}, bf16[1024,512]{1,0:T(8,128)(2,1)}, f32[1,1024]{1,0:T(1,128)}, bf16[8,16,1024]{2,1,0:T(8,128)(2,1)}) custom-call(bf16[128,576]{1,0:T(8,128)(2,1)} %pad_maximum_fusion.key_ref, bf16[1024,1024]{1,0:T(8,128)(2,1)} %select_bitcast_fusion.spread_ref, bf16[512,1024]{1,0:T(8,128)(2,1)} %weight_ref.1, ...), custom_call_target="tpu_custom_call" | custom-call | tf_op jit(solution)/shard_map/gather/pallas_call | solution.py:274
  34.2 14.1 %attend.1 = (bf16[1024,512]{1,0:T(8,128)(2,1)}, bf16[1024,64]{1,0:T(8,128)(2,1)}, bf16[1024,576]{1,0:T(8,128)(2,1)}) custom-call(bf16[1024,576]{1,0:T(8,128)(2,1)} %get-tuple-element.16.keys_ref, s32[1024,1]{1,0:T(8,128)} %add.57.posk_ref, s32[1,1024]{1,0:T(1,128)} %reshape_reshape.3.posq_ref, f32[1,1024]{1,0:T(1,128)} %get-tuple-element.17.delta_ref, ...), custom_call_target="tpu_custom_call" | custom-call | tf_op jit(solution)/shard_map/attend/pallas_call | solution.py:297
  48.2 1.8 %copy.22 = bf16[1,128,8,64]{1,3,2,0:T(8,128)(2,1)} copy(bf16[1,128,8,64]{3,2,1,0:T(8,128)(2,1)} %bitcast.18) | data formatting | bytes 262144
  50.0 60.3 %reduce.1 = (bf16[128,576]{1,0:T(8,128)(2,1)}, f32[224,576]{1,0:T(8,128)}, f32[16,1024]{1,0:T(8,128)}) custom-call(bf16[1024,576]{1,0:T(8,128)(2,1)} %get-tuple-element.21.term_ref, bf16[4,128,1792]{2,1,0:T(8,128)(2,1)} %layer_ref.1, bf16[8,16,1024]{2,1,0:T(8,128)(2,1)} %get-tuple-element.22.value_ref), custom_call_target="tpu_custom_call" | custom-call | tf_op jit(solution)/shard_map/reduce/pallas_call | solution.py:331
  110.3 0.8 slice_bitcast_fusion.1
  111.0 1.6 %slice_bitcast_fusion = bf16[1,128,512]{2,1,0:T(8,128)(2,1)} fusion(bf16[128,576]{1,0:T(8,128)(2,1)} %get-tuple-element.23), kind=kLoop, calls=%fused_computation.2 | loop fusion | bytes 262144 | tf_op jit(solution)/shard_map/broadcast_in_dim | solution.py:363
  112.6 0.7 copy.23
  113.3 1.9 %copy.26 = f32[224,576]{1,0:T(8,128)} copy(f32[224,576]{1,0:T(8,128)} %get-tuple-element.48) | data formatting | bytes 1032192
  115.2 1.5 %copy.27 = f32[16,1024]{1,0:T(8,128)} copy(f32[16,1024]{1,0:T(8,128)} %get-tuple-element.49) | data formatting | bytes 131072
  (2 shorter events, 0.0 us)

commit v2 on v1

--- a/solution.py
+++ b/solution.py
@@ -34,15 +34,17 @@
 
 def gather_kernel(
     n_dp, n_ctx,
-    key_ref, spread_ref, weight_ref, saved_ref,
+    lat_ref, rope_ref, out_ref, weight_ref, saved_ref,
     keys_ref, grad_ref, delta_ref, value_ref,
-    parts, landed, key_send, key_recv, pair_send, pair_recv, val_send, val_recv,
+    key_ref, spread_ref, parts, landed, key_send, key_recv, pair_send, pair_recv, val_send, val_recv,
 ):
     dp, ctx = lax.axis_index("dp"), lax.axis_index("ctx")
     n_z = n_ctx // 2
     z, core = ctx // 2, ctx % 2
-    tokens = key_ref.shape[0]
+    tokens, latent = lat_ref.shape
     partner = (dp, z * 2 + (1 - core))
+    key_ref[:, :latent] = lat_ref[...]
+    key_ref[:, latent:] = rope_ref[...]
     z_peer = lambda k: (dp, lax.rem(z + k, n_z) * 2 + core)
     dp_peer = lambda k: (lax.rem(dp + k, n_dp), ctx)
     greet(
@@ -62,6 +64,18 @@
     pair = remote(key_ref, rows_of(ctx), pair_send.at[0], pair_recv.at[0], partner)
     pair.start()
     keys_ref[pl.ds(pl.multiple_of(ctx * tokens, tokens), tokens), :] = key_ref[...]
+
+    heads = spread_ref.shape[0] // tokens
+    values = out_ref.shape[1]
+    lane = lax.broadcasted_iota(jnp.int32, (heads, values), 1)
+    head = lax.broadcasted_iota(jnp.int32, (heads, values), 0)
+    keep = (lane // (values // heads) == head)[None]
+    group = min(16, tokens)
+    for start in range(0, tokens, group):
+        piece = out_ref[start : start + group].astype(wide)
+        piece = jnp.broadcast_to(piece[:, None, :], (group, heads, values))
+        piece = jnp.where(keep, piece, 0.0).reshape(group * heads, values)
+        spread_ref[start * heads : (start + group) * heads, :] = piece.astype(low)
 
     share = parts.shape[1]
     value = dot(saved_ref[...], spread_ref[...], 0, 0).astype(low)
@@ -108,46 +122,11 @@
         copy.wait_send()
 
 
-def attend_kernel(
-    keys_ref, posk_ref, posq_ref, delta_ref, ql_ref, qr_ref, grad_ref,
-    dql_ref, dqr_ref, term_ref, total,
-):
-    step = pl.program_id(0)
-    latent = ql_ref.shape[1]
-    key_lat = keys_ref[:, :latent]
-    key_rope = keys_ref[:, latent:]
-    ql, qr, grad = ql_ref[...], qr_ref[...], grad_ref[...]
-    scores = (dot(key_lat, ql, 1, 1) + dot(key_rope, qr, 1, 1)) * softmax_scale
-    scores = jnp.where(posk_ref[...] <= posq_ref[...], scores, -jnp.inf)
-    top = jnp.max(scores, axis=0, keepdims=True)
-    expo = jnp.exp(scores - top)
-    probs = expo * (1.0 / jnp.sum(expo, axis=0, keepdims=True))
-    grad_prob = dot(key_lat, grad, 1, 1)
-    slope = (probs * (grad_prob - delta_ref[...])).astype(low)
-    dql_ref[...] = (softmax_scale * dot(slope, key_lat, 0, 0)).astype(low)
-    dqr_ref[...] = (softmax_scale * dot(slope, key_rope, 0, 0)).astype(low)
-    lat = dot(probs.astype(low), grad, 1, 0) + softmax_scale * dot(slope, ql, 1, 0)
-    rope = softmax_scale * dot(slope, qr, 1, 0)
-
-    @pl.when(step == 0)
-    def _():
-        total[:, :latent] = lat
-        total[:, latent:] = rope
-
-    @pl.when(step > 0)
-    def _():
-        total[:, :latent] += lat
-        total[:, latent:] += rope
-
-    @pl.when(step == pl.num_programs(0) - 1)
-    def _():
-        term_ref[...] = total[...].astype(low)
-
-
 def reduce_kernel(
     n_dp, n_ctx,
-    term_ref, layer_ref, value_ref,
-    joined_ref, down_ref, uv_ref,
+    blocks_ref, keys_ref, delta_ref, ql_ref, qr_ref, grad_ref, layer_ref, value_ref,
+    dql_ref, dqr_ref, joined_ref, down_ref, uv_ref,
+    posk, probs_all, slopes, chip_part, term_out,
     turned, pair_in, pair_sum, z_in, blocks_in, down_out, down_own, down_in, down_sum, down_z, value_in,
     a_send, a_recv, b_send, b_recv, c_send, c_recv, d_send, d_recv, e_send, e_recv, f_send, f_recv,
 ):
@@ -171,24 +150,66 @@
         pending.append(copy)
         return copy
 
-    def term_rows(index):
-        return pl.ds(pl.multiple_of(index * tokens, tokens), tokens)
-
-    first = {}
-    for k in order:
-        first[k] = send(
-            term_ref.at[term_rows(chip(k) * 2 + other)], pair_in.at[k], a_send.at[k], a_recv.at[k], partner
+    seq_rows = keys_ref.shape[0]
+    rows, latent = ql_ref.shape
+    heads = rows // tokens
+    half = tokens // 2
+    tile = min(256, rows)
+    for j in range(seq_rows // half):
+        posk[j * half : (j + 1) * half, :] = blocks_ref[j] * half + lax.broadcasted_iota(
+            jnp.int32, (half, 1), 0
         )
-    second = {}
-    mine = None
-    for k in order:
+    low_block, high_block = blocks_ref[2 * ctx], blocks_ref[2 * ctx + 1]
+
+    def score_tile(i, carry):
+        span = pl.ds(pl.multiple_of(i * tile, tile), tile)
+        token = (i * tile + lax.broadcasted_iota(jnp.int32, (1, tile), 1)) // heads
+        posq = jnp.where(token < half, low_block * half + token, high_block * half + token - half)
+        key_lat, key_rope = keys_ref[:, :latent], keys_ref[:, latent:]
+        scores = dot(key_lat, ql_ref[span, :], 1, 1) + dot(key_rope, qr_ref[span, :], 1, 1)
+        scores = jnp.where(posk[...] <= posq, scores * softmax_scale, -jnp.inf)
+        expo = jnp.exp(scores - jnp.max(scores, axis=0, keepdims=True))
+        probs = expo * (1.0 / jnp.sum(expo, axis=0, keepdims=True))
+        grad_prob = dot(key_lat, grad_ref[span, :], 1, 1)
+        probs_all[:, span] = probs.astype(low)
+        slopes[:, span] = (probs * (grad_prob - delta_ref[:, span])).astype(low)
+        return carry
+
+    lax.fori_loop(0, rows // tile, score_tile, 0)
+
+    first, second = {}, {}
+
+    def finish(at):
+        k, slot = order[at], at % 2
         first[k].wait_recv()
-        added = term_ref[term_rows(chip(k) * 2 + core), :].astype(wide) + pair_in[k].astype(wide)
+        added = chip_part[slot, pl.ds(pl.multiple_of(core * tokens, tokens), tokens), :] + pair_in[k].astype(wide)
         if k == 0:
-            mine = added
-        else:
-            pair_sum[k] = added.astype(low)
-            second[k] = send(pair_sum.at[k], z_in.at[k], b_send.at[k], b_recv.at[k], z_peer(k))
+            return added
+        pair_sum[k] = added.astype(low)
+        second[k] = send(pair_sum.at[k], z_in.at[k], b_send.at[k], b_recv.at[k], z_peer(k))
+
+    for at, k in enumerate(order):
+        span = pl.ds(pl.multiple_of(chip(k) * (2 * tokens), 2 * tokens), 2 * tokens)
+        slope = slopes[span, :]
+        slot = at % 2
+        chip_part[slot, :, :latent] = dot(probs_all[span, :], grad_ref[...], 1, 0) + softmax_scale * dot(
+            slope, ql_ref[...], 1, 0
+        )
+        chip_part[slot, :, latent:] = softmax_scale * dot(slope, qr_ref[...], 1, 0)
+        term_out[k] = chip_part[slot, pl.ds(pl.multiple_of(other * tokens, tokens), tokens), :].astype(low)
+        first[k] = send(term_out.at[k], pair_in.at[k], a_send.at[k], a_recv.at[k], partner)
+        if at > 0:
+            finish(at - 1)
+    mine = finish(n_z - 1)
+
+    def query_tile(i, carry):
+        span = pl.ds(pl.multiple_of(i * tile, tile), tile)
+        slope = slopes[:, span]
+        dql_ref[span, :] = (softmax_scale * dot(slope, keys_ref[:, :latent], 0, 0)).astype(low)
+        dqr_ref[span, :] = (softmax_scale * dot(slope, keys_ref[:, latent:], 0, 0)).astype(low)
+        return carry
+
+    lax.fori_loop(0, rows // tile, query_tile, 0)
     batch = layer_ref.shape[0]
     for d in range(batch):
         turned[:, d * tokens : (d + 1) * tokens] = layer_ref[d].T
@@ -251,7 +272,6 @@
     heads, latent = q_latent.shape[2], q_latent.shape[3]
     rope_width = key_rope.shape[2]
     width = latent + rope_width
-    value_width = w_uv.shape[1] // heads
     seq_rows = half_rows * blocks.shape[0]
     rows = tokens * heads
     n_z = n_ctx // 2
@@ -259,18 +279,7 @@
     vmem = pl.BlockSpec(memory_space=pltpu.VMEM)
     dma = lambda n: pltpu.SemaphoreType.DMA((n,))
 
-    keys = jnp.concatenate([kv_latent[0], key_rope[0]], axis=1)
-    head_of = jnp.arange(values, dtype=jnp.int32) // value_width
-    keep = head_of[None, :] == jnp.arange(heads, dtype=jnp.int32)[:, None]
-    spread = jnp.where(keep[None], d_out[0][:, None, :], jnp.zeros((), low)).reshape(rows, values)
     saved = saved_output[0].reshape(rows, latent)
-    offsets = jnp.arange(half_rows, dtype=jnp.int32)
-    pos_key = (blocks[:, None] * half_rows + offsets[None, :]).reshape(seq_rows, 1)
-    own_blocks = lax.dynamic_slice_in_dim(blocks, 2 * lax.axis_index("ctx"), 2, 0)
-    pos_query = jnp.repeat(
-        (own_blocks[:, None] * half_rows + offsets[None, :]).reshape(tokens), heads
-    ).reshape(1, rows)
-
     all_keys, grad, delta, value_sum = pl.pallas_call(
         functools.partial(gather_kernel, n_dp, n_ctx),
         out_shape=(
@@ -279,9 +288,11 @@
             jax.ShapeDtypeStruct((1, rows), wide),
             jax.ShapeDtypeStruct((n_ctx, latent // (n_dp * n_ctx), values), low),
         ),
-        in_specs=[vmem] * 4,
+        in_specs=[vmem] * 5,
         out_specs=(vmem,) * 4,
         scratch_shapes=[
+            pltpu.VMEM((tokens, width), low),
+            pltpu.VMEM((rows, values), low),
             pltpu.VMEM((n_dp, latent // n_dp, values), low),
             pltpu.VMEM((n_dp, latent // n_dp, values), low),
             dma(n_z), dma(n_z), dma(n_z), dma(n_z), dma(n_dp), dma(n_dp),
@@ -290,54 +301,27 @@
             collective_id=0, has_side_effects=True, vmem_limit_bytes=VMEM_LIMIT
         ),
         name="gather",
-    )(keys, spread, w_uv, saved)
-
-    tile = min(256, rows)
-    whole = lambda shape: pl.BlockSpec(shape, lambda i: (0, 0))
-    d_lat, d_rope, term = pl.pallas_call(
-        attend_kernel,
-        grid=(rows // tile,),
+    )(kv_latent[0], key_rope[0], d_out[0], w_uv, saved)
+
+    height = layer_input.shape[2] // n_ctx
+    batch = layer_input.shape[0]
+    d_lat, d_rope, joined, grad_down, grad_uv = pl.pallas_call(
+        functools.partial(reduce_kernel, n_dp, n_ctx),
         out_shape=(
             jax.ShapeDtypeStruct((rows, latent), low),
             jax.ShapeDtypeStruct((rows, rope_width), low),
-            jax.ShapeDtypeStruct((seq_rows, width), low),
-        ),
-        in_specs=[
-            whole((seq_rows, width)),
-            whole((seq_rows, 1)),
-            pl.BlockSpec((1, tile), lambda i: (0, i)),
-            pl.BlockSpec((1, tile), lambda i: (0, i)),
-            pl.BlockSpec((tile, latent), lambda i: (i, 0)),
-            pl.BlockSpec((tile, rope_width), lambda i: (i, 0)),
-            pl.BlockSpec((tile, latent), lambda i: (i, 0)),
-        ],
-        out_specs=(
-            pl.BlockSpec((tile, latent), lambda i: (i, 0)),
-            pl.BlockSpec((tile, rope_width), lambda i: (i, 0)),
-            whole((seq_rows, width)),
-        ),
-        scratch_shapes=[pltpu.VMEM((seq_rows, width), wide)],
-        compiler_params=pltpu.CompilerParams(
-            dimension_semantics=("arbitrary",), vmem_limit_bytes=VMEM_LIMIT
-        ),
-        name="attend",
-    )(
-        all_keys, pos_key, pos_query, delta,
-        q_latent[0].reshape(rows, latent), q_rope[0].reshape(rows, rope_width), grad,
-    )
-
-    height = layer_input.shape[2] // n_ctx
-    batch = layer_input.shape[0]
-    joined, grad_down, grad_uv = pl.pallas_call(
-        functools.partial(reduce_kernel, n_dp, n_ctx),
-        out_shape=(
             jax.ShapeDtypeStruct((tokens, width), low),
             jax.ShapeDtypeStruct((height, width), wide),
             jax.ShapeDtypeStruct((latent // (n_dp * n_ctx), values), wide),
         ),
-        in_specs=[vmem] * 3,
-        out_specs=(vmem,) * 3,
+        in_specs=[pl.BlockSpec(memory_space=pltpu.SMEM)] + [vmem] * 7,
+        out_specs=(vmem,) * 5,
         scratch_shapes=[
+            pltpu.VMEM((seq_rows, 1), jnp.int32),
+            pltpu.VMEM((seq_rows, rows), low),
+            pltpu.VMEM((seq_rows, rows), low),
+            pltpu.VMEM((2, 2 * tokens, width), wide),
+            pltpu.VMEM((n_z, tokens, width), low),
             pltpu.VMEM((layer_input.shape[2], batch * tokens), low),
             pltpu.VMEM((n_z, tokens, width), low),
             pltpu.VMEM((n_z, tokens, width), low),
@@ -356,7 +340,11 @@
             collective_id=1, has_side_effects=True, vmem_limit_bytes=VMEM_LIMIT
         ),
         name="reduce",
-    )(term, layer_input, value_sum)
+    )(
+        blocks, all_keys, delta,
+        q_latent[0].reshape(rows, latent), q_rope[0].reshape(rows, rope_width),
+        grad, layer_input, value_sum,
+    )
     return (
         d_lat.reshape(1, tokens, heads, latent),
         d_rope.reshape(1, tokens, heads, rope_width),

time: 117 us -> 104 us (0.89)
  Pallas kernels: 97.4 us -> 91.5 us
  other arithmetic: 5.69 us -> 0 us
    pallas_call x1 -> x0, Pallas kernels: 14.1 us -> none  [body(): pl.pallas_call(attend_kernel, grid=(rows // tile,), out_shape=(jax.ShapeD...]
    pallas_call x1, Pallas kernels: 60.3 us -> 68.9 us  [body(): pl.pallas_call(functools.partial(reduce_kernel, n_dp, n_ctx), out_shape=(...]
    select_n x2 -> x0, other arithmetic: 2.56 us -> none  [the longest x1 2.56 us: body(): jnp.where(keep[None], d_out[0][:, None, :], jnp.zeros((), low))]
    concatenate x1 -> x0, other arithmetic: 1.58 us -> none  [body(): keys = jnp.concatenate([kv_latent[0], key_rope[0]], axis=1)]
    mul x2 -> x0, other arithmetic: 1.39 us -> none  [the longest x1 0.73 us: body(): own_blocks[:, None] * half_rows + offsets[None, :]]
    add x2 -> x0, local copies, waits for them, and re-layouts: 1.35 us -> none  [the longest x1 1.26 us: body(): blocks[:, None] * half_rows + offsets[None, :]]
    unnamed x6 -> x11, local copies, waits for them, and re-layouts: 8.43 us -> 9.44 us
where the time goes in v2:
time: 104 us
  Pallas kernels  91.5 us (88%)
  local copies, waits for them, and re-layouts  11.8 us (11%)
    pallas_call x1, Pallas kernels, body(): pl.pallas_call(functools.partial(reduce_kernel, n_dp, n_ctx), out_shape=(...  68.9 us
    pallas_call x1, Pallas kernels, body(): pl.pallas_call(functools.partial(gather_kernel, n_dp, n_ctx), out_shape=(...  22.6 us
    unnamed x11, local copies, waits for them, and re-layouts  9.44 us

profile of v2, /device:TPU:27, one launch (start us, length us, event | category | flops | bytes accessed | tf_op | source)
XLA Modules:
  0.0 104.0 jit_solution(11402013166499354364)
XLA Ops:
  0.6 1.4 %copy.15 = bf16[1,128,64]{2,1,0:T(8,128)(2,1)} copy(bf16[1,128,64]{1,2,0:T(8,128)(2,1)} %param.11) | data formatting | bytes 32768 | tf_op args[2]
  2.1 1.8 %copy.16 = bf16[1,128,8,64]{3,2,1,0:T(8,128)(2,1)} copy(bf16[1,128,8,64]{1,3,2,0:T(8,128)(2,1)} %param.13) | data formatting | bytes 262144 | tf_op args[4]
  3.8 22.6 %gather.1 = (bf16[1024,576]{1,0:T(8,128)(2,1)}, bf16[1024,512]{1,0:T(8,128)(2,1)}, f32[1,1024]{1,0:T(1,128)}, bf16[8,16,1024]{2,1,0:T(8,128)(2,1)}) custom-call(bf16[128,512]{1,0:T(8,128)(2,1)} %bitcast.19, bf16[128,64]{1,0:T(8,128)(2,1)} %bitcast.18, bf16[128,1024]{1,0:T(8,128)(2,1)} %bitcast.16, bf16[512,1024]{1,0:T(8,128)(2,1)} %weight_ref.1, ...), custom_call_target="tpu_custom_call" | custom-call | tf_op jit(solution)/shard_map/gather/pallas_call | solution.py:283
  26.4 68.9 %reduce.1 = (bf16[1024,512]{1,0:T(8,128)(2,1)}, bf16[1024,64]{1,0:T(8,128)(2,1)}, bf16[128,576]{1,0:T(8,128)(2,1)}, f32[224,576]{1,0:T(8,128)}, f32[16,1024]{1,0:T(8,128)}) custom-call(s32[16]{0:T(128)} %blocks_ref.1, bf16[1024,576]{1,0:T(8,128)(2,1)} %get-tuple-element.15.keys_ref, f32[1,1024]{1,0:T(1,128)} %get-tuple-element.16.delta_ref, ...), custom_call_target="tpu_custom_call" | custom-call | tf_op jit(solution)/shard_map/reduce/pallas_call | solution.py:308
  95.4 0.0 copy-start
  95.4 1.8 %copy.17 = bf16[1,128,8,64]{1,3,2,0:T(8,128)(2,1)} copy(bf16[1,128,8,64]{3,2,1,0:T(8,128)(2,1)} %bitcast.17) | data formatting | bytes 262144
  97.2 0.0 copy-start.1
  97.2 0.8 slice_bitcast_fusion.1
  98.0 1.6 %slice_bitcast_fusion = bf16[1,128,512]{2,1,0:T(8,128)(2,1)} fusion(bf16[128,576]{1,0:T(8,128)(2,1)} %get-tuple-element.21), kind=kLoop, calls=%fused_computation | loop fusion | bytes 262144 | tf_op jit(solution)/shard_map/broadcast_in_dim | solution.py:351
  99.6 0.7 copy.18
  100.3 2.3 %copy.22 = bf16[1,128,8,512]{3,2,1,0:T(8,128)(2,1)} copy(bf16[1,128,8,512]{3,2,1,0:T(8,128)(2,1)} %bitcast.13) | data formatting | bytes 2097152
  102.5 0.0 copy-done
  102.5 0.8 copy.23
  103.4 0.0 copy-done.1
  103.4 0.6 copy.24
Async XLA Ops:
  95.4 7.2 %copy-start = (f32[224,576]{1,0:T(8,128)S(1)}, f32[224,576]{1,0:T(8,128)}, u32[]{:S(2)}) copy-start(f32[224,576]{1,0:T(8,128)} %get-tuple-element.40) | copy-start | bytes 1548292
  97.2 6.1 %copy-start.1 = (f32[16,1024]{1,0:T(8,128)S(1)}, f32[16,1024]{1,0:T(8,128)}, u32[]{:S(2)}) copy-start(f32[16,1024]{1,0:T(8,128)} %get-tuple-element.41) | copy-start | bytes 196612
